TPU v7x, 256 devices: a whole 4x4x8 slice. The times are simulated.
256 devices in a mesh: row: 8 (over z_lo, y), col: 32 (over z_hi, x, core).
Axes of the slice: x: 4, y: 4, z: 8 (z_hi: 4, z_lo: 2; z = z_hi * 2 + z_lo), core: 2. Of those that a mesh axis runs over, the one named last changes fastest.
Arguments:
- alignment: float32 [512, 768, 256], P('row', 'col'), may hold values from -40 to 40
- seq_mask: int32 [512], replicated, may hold values 0 or 1
- res_mask: int32 [768], replicated, may hold values 0 or 1
- attn_gain: float32 [256], replicated, may hold values from 0.5 to 1.5
- outer_product_gain: float32 [256], replicated, may hold values from 0.5 to 1.5
- w_query: bfloat16 [256, 256], replicated, may hold values from -24 to 24
- w_key: bfloat16 [256, 256], replicated, may hold values from -2 to 2
- w_value: bfloat16 [256, 256], replicated, may hold values from -0.375 to 0.375
- w_gate: bfloat16 [256, 256], replicated, may hold values from -0.375 to 0.375
- output_weight: bfloat16 [256, 256], replicated, may hold values from -0.375 to 0.375
- w_left: bfloat16 [256, 32], replicated, may hold values from -0.375 to 0.375
- w_right: bfloat16 [256, 32], replicated, may hold values from -0.375 to 0.375
- w_pair: bfloat16 [1024, 128], replicated, may hold values from -3 to 3
Outputs:
- alignment_output: float32 [512, 768, 256], P('row', 'col')
- pair_increment: float32 [768, 768, 128], P('row', 'col')
All inputs are finite; a program needn't handle non-finite values.
Results may differ from a plain program's by a relative error of at most 0.0095.
Values may be sent and summed in bfloat16 or wider, within the bound.
No kernel may reach another device: no remote copies, remote signals or barrier semaphores. Data moves between devices by JAX's collectives and lax.ppermute only.
A program may use at most 128 MiB of HBM per device.

v0:
```python
import jax
import jax.numpy as jnp
from jax import lax
from jax.sharding import PartitionSpec as P

HEADS = 8
HEAD_DIM = 32


def sent_to_all(shard, axis):
    copies = jnp.broadcast_to(shard, (lax.axis_size(axis), *shard.shape))
    return lax.all_to_all(copies, axis, split_axis=0, concat_axis=0, tiled=True)


def laid_out(blocks, dim):
    blocks = jnp.moveaxis(blocks, 0, dim)
    shape = blocks.shape
    return blocks.reshape(*shape[:dim], shape[dim] * shape[dim + 1], *shape[dim + 2 :])


def gathered_copies(shard, axis, dim):
    blocks = sent_to_all(shard, axis)
    return laid_out(blocks, dim)


def normalized_rows(values, gains):
    average = jnp.mean(values, -1, keepdims=True)
    centred = values - average
    spread = jnp.mean(centred * centred, -1, keepdims=True)
    return centred * lax.rsqrt(spread + 1e-05) * gains


def shards(
    alignment,
    seq_mask,
    res_mask,
    attn_gain,
    outer_product_gain,
    w_query,
    w_key,
    w_value,
    w_gate,
    output_weight,
    w_left,
    w_right,
    w_pair,
):
    seq_dev, res_dev, channel_width = alignment.shape
    row_count = lax.axis_size("row")
    col_count = lax.axis_size("col")
    sequence_total = seq_mask.shape[0]
    hidden = w_query.shape[1]
    query_scale = HEAD_DIM ** (-0.5)
    key_bias = jnp.where(seq_mask > 0, 0.0, -1000000000.0).astype(jnp.float32)
    normed = normalized_rows(alignment, attn_gain).astype(jnp.bfloat16)
    normed = normed.reshape(seq_dev, row_count, res_dev // row_count, channel_width)

    def column(column_parts):
        col_query, col_key, col_value, col_gate = column_parts
        heads_query = col_query.reshape(sequence_total, HEADS, HEAD_DIM)
        heads_key = col_key.reshape(sequence_total, HEADS, HEAD_DIM)
        heads_value = col_value.reshape(sequence_total, HEADS, HEAD_DIM)
        logits = (
            jnp.einsum("shd,thd->hst", heads_query, heads_key, preferred_element_type=jnp.float32)
            + key_bias[None, None, :]
        )
        weights = jax.nn.softmax(logits, axis=-1).astype(jnp.bfloat16)
        attended = jnp.einsum(
            "hst,thd->shd", weights, heads_value, preferred_element_type=jnp.float32
        ).reshape(sequence_total, hidden)
        return (jax.nn.sigmoid(col_gate) * attended).astype(jnp.bfloat16)

    tokens = lax.all_to_all(normed, "row", split_axis=1, concat_axis=0, tiled=True)[:, 0]
    residues = tokens.shape[1]
    token_rows = tokens.reshape(-1, channel_width)
    queries = (
        jnp.dot(token_rows, w_query, preferred_element_type=jnp.float32) * query_scale
    ).astype(jnp.bfloat16)
    key_rows = jnp.dot(token_rows, w_key, preferred_element_type=jnp.float32).astype(jnp.bfloat16)
    value_rows = jnp.dot(token_rows, w_value, preferred_element_type=jnp.float32).astype(
        jnp.bfloat16
    )
    gate_lin = jnp.dot(token_rows, w_gate, preferred_element_type=jnp.float32)

    def arrange(values):
        return values.reshape(sequence_total, residues, -1).transpose(1, 0, 2)

    gated_output = lax.map(
        column, (arrange(queries), arrange(key_rows), arrange(value_rows), arrange(gate_lin))
    )
    gated_output = gated_output.transpose(1, 0, 2)[:, None]
    returned_value = lax.all_to_all(gated_output, "row", split_axis=0, concat_axis=1, tiled=True)
    returned_value = returned_value.reshape(-1, hidden)
    alignment_output = alignment + jnp.dot(
        returned_value, output_weight, preferred_element_type=jnp.float32
    ).reshape(seq_dev, res_dev, channel_width)
    row_index = lax.axis_index("row")
    col_index = lax.axis_index("col")
    side_width = w_left.shape[1]
    second_normalized = (
        normalized_rows(alignment_output, outer_product_gain)
        .astype(jnp.bfloat16)
        .reshape(-1, channel_width)
    )
    own_seq = lax.dynamic_slice_in_dim(seq_mask, row_index * seq_dev, seq_dev, 0)
    own_res = lax.dynamic_slice_in_dim(res_mask, col_index * res_dev, res_dev, 0)
    side_mask = (own_seq[:, None] * own_res[None, :]).astype(jnp.float32)[:, :, None]
    left = (
        (
            jnp.dot(second_normalized, w_left, preferred_element_type=jnp.float32).reshape(
                seq_dev, res_dev, side_width
            )
            * side_mask
        )
        .astype(jnp.bfloat16)
        .reshape(seq_dev, -1)
    )
    right = (
        (
            jnp.dot(second_normalized, w_right, preferred_element_type=jnp.float32).reshape(
                seq_dev, res_dev, side_width
            )
            * side_mask
        )
        .astype(jnp.bfloat16)
        .reshape(seq_dev, -1)
    )
    pair_rows = res_dev * col_count // row_count
    contraction = (((0,), (0,)), ((), ()))
    right_all = gathered_copies(right, "row", 0)
    group = seq_dev // col_count
    right_order = (
        right_all.reshape(row_count, col_count, group, -1)
        .transpose(1, 0, 2, 3)
        .reshape(sequence_total, -1)
    )
    spread_out = lax.all_to_all(left, "col", split_axis=0, concat_axis=1, tiled=True)
    own_block = lax.all_to_all(spread_out, "row", split_axis=1, concat_axis=0, tiled=True)
    products = lax.dot_general(
        lax.all_gather(own_block, "col", axis=0, tiled=True),
        right_order,
        contraction,
        preferred_element_type=jnp.float32,
    )
    outer_sum = (
        products.reshape(pair_rows, side_width, res_dev, side_width)
        .transpose(0, 2, 1, 3)
        .reshape(-1, side_width * side_width)
        .astype(jnp.bfloat16)
    )
    projected_output = jnp.dot(outer_sum, w_pair, preferred_element_type=jnp.float32).reshape(
        pair_rows, res_dev, -1
    )
    pair_res = lax.dynamic_slice_in_dim(res_mask, row_index * pair_rows, pair_rows, 0)
    live_total = jnp.sum(seq_mask)
    count_values = jnp.maximum(live_total * pair_res[:, None] * own_res[None, :], 1).astype(
        jnp.float32
    )
    return (alignment_output, projected_output / count_values[:, :, None])


def solution(mesh):
    in_specs = (P("row", "col", None), P(), P(), P(), P(), P(), P(), P(), P(), P(), P(), P(), P())
    out_specs = (P("row", "col", None), P("row", "col", None))
    return jax.shard_map(shards, mesh=mesh, in_specs=in_specs, out_specs=out_specs, check_vma=False)
```

profile of v0, /device:TPU:5, one launch (start us, length us, event | category | flops | bytes accessed | tf_op | source)
XLA Modules:
  0.0 247.4 jit_solution(861617664489180695)
XLA Ops:
  7.2 1.8 reduce_sum.54
  9.9 1.5 multiply_convert_fusion.1
  11.4 5.5 %all-to-all-start = ((bf16[64,8,3,256]{3,0,2,1:T(8,128)(2,1)}), bf16[64,8,3,256]{3,0,2,1:T(8,128)(2,1)S(1)}, u32[]{:S(2)}, u32[]{:S(2)}) async-start(bf16[64,8,3,256]{3,0,2,1:T(8,128)(2,1)} %bitcast.5), calls=%async_computation | async-start | bytes 1572864 | tf_op jit(solution)/shard_map/all_to_all | solution.py:73
  17.0 11.5 %all-to-all-done = bf16[64,8,3,256]{3,0,2,1:T(8,128)(2,1)S(1)} async-done(((bf16[64,8,3,256]{3,0,2,1:T(8,128)(2,1)}), bf16[64,8,3,256]{3,0,2,1:T(8,128)(2,1)S(1)}, u32[]{:S(2)}, u32[]{:S(2)}) %all-to-all-start) | async-done | bytes 786464 | tf_op jit(solution)/shard_map/all_to_all | solution.py:73
  28.5 1.6 copy.99
  31.1 2.4 reshape_squeeze.3
  35.1 2.3 copy.101
  38.9 2.3 copy.102
  42.5 2.5 reshape.159
  44.9 1.6 copy.103
  46.6 2.6 %convolution_bitcast_fusion = f32[3,512,256]{2,1,0:T(8,128)} fusion(bf16[512,3,256]{2,0,1:T(8,128)(2,1)} %bitcast.103, bf16[256,256]{1,0:T(8,128)(2,1)S(1)} %copy-done.3), kind=kOutput, calls=%fused_computation.25 | convolution fusion | flops 201326592 | bytes 2490368 | tf_op jit(solution)/shard_map/dot_general | solution.py:83
  49.2 40.3 %while.10 = (s32[]{:T(128)}, bf16[3,512,256]{1,2,0:T(8,128)(2,1)}, f32[3,512,256]{2,1,0:T(8,128)}, bf16[3,512,256]{1,2,0:T(8,128)(2,1)}, bf16[3,512,256]{1,2,0:T...) while((s32[]{:T(128)}, bf16[3,512,256]{1,2,0:T(8,128)(2,1)}, ...), condition=%wide.region_5.6_spmd, body=%wide.region_2.5_spmd.sunk | while | flops 279577088 | bytes 23104096 | solution.py:88
  50.3 5.0 %fusion.43 = (f32[8,512]{1,0:T(8,128)S(1)}, f32[8,512,512]{1,2,0:T(8,128)}) fusion(f32[512]{0:T(512)S(1)} %get-tuple-element.174, bf16[512,8,32]{0,2,1:T(8,128)(2,1)S(1)} %bitcast.97, bf16[512,8,32]{0,2,1:T(8,128)(2,1)S(1)} %bitcast.96), kind=kOutput, calls=%fused_computation.46.clone.1 | convolution fusion | flops 140509696 | bytes 8931328 | tf_op jit(solution)/shard_map/while/body/eval_jaxpr/sub | solution.py:67
  56.3 4.2 %fusion.44 = f32[8,32,512]{2,1,0:T(8,128)S(1)} fusion(bf16[512,8,32]{0,2,1:T(8,128)(2,1)S(1)} %bitcast.95, f32[8,512,512]{1,2,0:T(8,128)} %get-tuple-element.150, f32[8,512]{1,0:T(8,128)S(1)} %get-tuple-element.151), kind=kOutput, calls=%fused_computation.6.clone.1 | convolution fusion | flops 138412032 | bytes 9191424 | tf_op jit(solution)/shard_map/while/body/eval_jaxpr/hst,thd->shd/dot_general | solution.py:68
  63.7 5.0 %fusion.43 = (f32[8,512]{1,0:T(8,128)S(1)}, f32[8,512,512]{1,2,0:T(8,128)}) fusion(f32[512]{0:T(512)S(1)} %get-tuple-element.174, bf16[512,8,32]{0,2,1:T(8,128)(2,1)S(1)} %bitcast.97, bf16[512,8,32]{0,2,1:T(8,128)(2,1)S(1)} %bitcast.96), kind=kOutput, calls=%fused_computation.46.clone.1 | convolution fusion | flops 140509696 | bytes 8931328 | tf_op jit(solution)/shard_map/while/body/eval_jaxpr/sub | solution.py:67
  69.7 4.2 %fusion.44 = f32[8,32,512]{2,1,0:T(8,128)S(1)} fusion(bf16[512,8,32]{0,2,1:T(8,128)(2,1)S(1)} %bitcast.95, f32[8,512,512]{1,2,0:T(8,128)} %get-tuple-element.150, f32[8,512]{1,0:T(8,128)S(1)} %get-tuple-element.151), kind=kOutput, calls=%fused_computation.6.clone.1 | convolution fusion | flops 138412032 | bytes 9191424 | tf_op jit(solution)/shard_map/while/body/eval_jaxpr/hst,thd->shd/dot_general | solution.py:68
  77.1 5.0 %fusion.43 = (f32[8,512]{1,0:T(8,128)S(1)}, f32[8,512,512]{1,2,0:T(8,128)}) fusion(f32[512]{0:T(512)S(1)} %get-tuple-element.174, bf16[512,8,32]{0,2,1:T(8,128)(2,1)S(1)} %bitcast.97, bf16[512,8,32]{0,2,1:T(8,128)(2,1)S(1)} %bitcast.96), kind=kOutput, calls=%fused_computation.46.clone.1 | convolution fusion | flops 140509696 | bytes 8931328 | tf_op jit(solution)/shard_map/while/body/eval_jaxpr/sub | solution.py:67
  83.1 4.2 %fusion.44 = f32[8,32,512]{2,1,0:T(8,128)S(1)} fusion(bf16[512,8,32]{0,2,1:T(8,128)(2,1)S(1)} %bitcast.95, f32[8,512,512]{1,2,0:T(8,128)} %get-tuple-element.150, f32[8,512]{1,0:T(8,128)S(1)} %get-tuple-element.151), kind=kOutput, calls=%fused_computation.6.clone.1 | convolution fusion | flops 138412032 | bytes 9191424 | tf_op jit(solution)/shard_map/while/body/eval_jaxpr/hst,thd->shd/dot_general | solution.py:68
  89.5 2.3 copy.104
  91.8 4.3 %all-to-all-start.1 = ((bf16[512,1,3,256]{3,2,1,0:T(4,128)(2,1)}), bf16[512,1,3,256]{3,2,1,0:T(4,128)(2,1)S(1)}, u32[]{:S(2)}, u32[]{:S(2)}) async-start(bf16[512,1,3,256]{3,2,1,0:T(4,128)(2,1)} %bitcast.102), calls=%async_computation.1 | async-start | bytes 2097152 | tf_op jit(solution)/shard_map/all_to_all | solution.py:92
  97.0 14.0 %all-to-all-done.1 = bf16[512,1,3,256]{3,2,1,0:T(4,128)(2,1)S(1)} async-done(((bf16[512,1,3,256]{3,2,1,0:T(4,128)(2,1)}), bf16[512,1,3,256]{3,2,1,0:T(4,128)(2,1)S(1)}, u32[]{:S(2)}, u32[]{:S(2)}) %all-to-all-start.1) | async-done | bytes 786464 | tf_op jit(solution)/shard_map/all_to_all | solution.py:92
  114.8 19.5 %all_to_all.70 = bf16[32,2,768]{2,1,0:T(2,128)(2,1)S(1)} all-to-all(bf16[32,2,768]{2,1,0:T(2,128)(2,1)S(1)} %all_to_all.57), channel_id=1, replica_groups=mesh['row'=8,'col'=32] {'col'}, dimensions={0} | all-to-all | bytes 196608 | tf_op jit(solution)/shard_map/all_to_all | solution.py:137
  134.3 8.1 %all_to_all.71 = bf16[2,8,3072]{2,0,1:T(2,128)(2,1)S(1)} all-to-all(bf16[2,8,3072]{2,0,1:T(2,128)(2,1)S(1)} %bitcast.112), channel_id=1, replica_groups=mesh['row'=8,'col'=32] {'row'}, dimensions={1} | all-to-all | bytes 196608 | tf_op jit(solution)/shard_map/all_to_all | solution.py:138
  145.3 3.5 %all-to-all-start.4 = ((bf16[8,64,768]{2,1,0:T(8,128)(2,1)}), bf16[8,64,768]{2,1,0:T(8,128)(2,1)S(1)}, u32[]{:S(2)}, u32[]{:S(2)}) async-start(bf16[8,64,768]{2,1,0:T(8,128)(2,1)} %broadcast_in_dim.23), calls=%async_computation.4 | async-start | bytes 1572864 | tf_op jit(solution)/shard_map/all_to_all | solution.py:12
  149.5 1.4 dynamic-slice_multiply_fusion
  151.0 8.0 %all-to-all-done.4 = bf16[8,64,768]{2,1,0:T(8,128)(2,1)S(1)} async-done(((bf16[8,64,768]{2,1,0:T(8,128)(2,1)}), bf16[8,64,768]{2,1,0:T(8,128)(2,1)S(1)}, u32[]{:S(2)}, u32[]{:S(2)}) %all-to-all-start.4) | async-done | bytes 786464 | tf_op jit(solution)/shard_map/all_to_all | solution.py:12
  161.6 35.4 %all-gather.2.cloned.1.call-done = bf16[512,3072]{1,0:T(8,128)(2,1)} async-done(((bf16[16,3072]{1,0:T(8,128)(2,1)}), bf16[512,3072]{1,0:T(8,128)(2,1)}) %all-gather.2.cloned.1.call-update) | async-done | bytes 3145744 | tf_op jit(solution)/shard_map/all_gather | solution.py:140
  197.0 3.2 %copy.114 = bf16[3072,512]{1,0:T(8,128)(2,1)S(1)} copy(bf16[3072,512]{0,1:T(8,128)(2,1)} %bitcast.105) | data formatting | bytes 6291456 | tf_op jit(solution)/shard_map/dot_general | solution.py:139
  200.2 13.7 %convert_bitcast_fusion = bf16[96,24,32,32]{3,2,1,0:T(8,128)(2,1)} fusion(bf16[96,32,512,1]{2,1,3,0:T(8,128)(2,1)S(1)} %bitcast.106, bf16[24,32,512,1]{2,1,0,3:T(8,128)(2,1)} %bitcast.110), kind=kOutput, calls=%fused_computation.15 | convolution fusion | flops 2418278400 | bytes 8650752 | tf_op jit(solution)/shard_map/dot_general | solution.py:139
  213.9 20.1 %copy.120 = bf16[96,24,32,32]{0,3,2,1:T(8,128)(2,1)} copy(bf16[96,24,32,32]{3,2,1,0:T(8,128)(2,1)} %convert_bitcast_fusion) | data formatting | bytes 9437184 | tf_op jit(solution)/shard_map/convert_element_type | solution.py:149
  234.1 4.8 %convolution_divide_fusion = f32[96,24,128]{2,0,1:T(8,128)S(1)} fusion(bf16[96,24,1024]{0,2,1:T(8,128)(2,1)} %bitcast.98, f32[96,24]{0,1:T(8,128)S(1)} %maximum_convert_fusion, bf16[1024,128]{1,0:T(8,128)(2,1)S(1)} %copy-done), kind=kOutput, calls=%fused_computation.27 | convolution fusion | flops 604274688 | bytes 6169600 | tf_op jit(solution)/shard_map/dot_general | solution.py:151
  238.9 1.7 copy.122
  (81 shorter events, 29.5 us)
Async XLA Ops:
  7.2 226.9 %copy-start = (bf16[1024,128]{1,0:T(8,128)(2,1)S(1)}, bf16[1024,128]{1,0:T(8,128)(2,1)}, u32[]{:S(2)}) copy-start(bf16[1024,128]{1,0:T(8,128)(2,1)} %param.27) | copy-start | bytes 786436
  7.2 1.9 copy-start.1
  7.2 2.7 %copy-start.9 = (f32[256]{0:T(256)S(1)}, f32[256]{0:T(256)}, u32[]{:S(2)}) copy-start(f32[256]{0:T(256)} %param.18) | copy-start | bytes 3076
  9.9 7.0 %copy-start.8 = (s32[512]{0:T(512)S(1)}, s32[512]{0:T(512)}, u32[]{:S(2)}) copy-start(s32[512]{0:T(512)} %param.16) | copy-start | bytes 6148
  11.4 17.1 %all-to-all-start = ((bf16[64,8,3,256]{3,0,2,1:T(8,128)(2,1)}), bf16[64,8,3,256]{3,0,2,1:T(8,128)(2,1)S(1)}, u32[]{:S(2)}, u32[]{:S(2)}) async-start(bf16[64,8,3,256]{3,0,2,1:T(8,128)(2,1)} %bitcast.5), calls=%async_computation | async-start | bytes 1572864 | tf_op jit(solution)/shard_map/all_to_all | solution.py:73
  30.1 3.4 %copy-start.5 = (bf16[256,256]{1,0:T(8,128)(2,1)S(1)}, bf16[256,256]{1,0:T(8,128)(2,1)}, u32[]{:S(2)}) copy-start(bf16[256,256]{1,0:T(8,128)(2,1)} %param.22) | copy-start | bytes 393220
  33.9 3.5 %copy-start.6 = (bf16[256,256]{1,0:T(8,128)(2,1)S(1)}, bf16[256,256]{1,0:T(8,128)(2,1)}, u32[]{:S(2)}) copy-start(bf16[256,256]{1,0:T(8,128)(2,1)} %param.20) | copy-start | bytes 393220
  37.7 3.5 %copy-start.7 = (bf16[256,256]{1,0:T(8,128)(2,1)S(1)}, bf16[256,256]{1,0:T(8,128)(2,1)}, u32[]{:S(2)}) copy-start(bf16[256,256]{1,0:T(8,128)(2,1)} %param.21) | copy-start | bytes 393220
  42.5 4.1 %copy-start.3 = (bf16[256,256]{1,0:T(8,128)(2,1)S(1)}, bf16[256,256]{1,0:T(8,128)(2,1)}, u32[]{:S(2)}) copy-start(bf16[256,256]{1,0:T(8,128)(2,1)} %param.23) | copy-start | bytes 393220
  91.8 19.2 %all-to-all-start.1 = ((bf16[512,1,3,256]{3,2,1,0:T(4,128)(2,1)}), bf16[512,1,3,256]{3,2,1,0:T(4,128)(2,1)S(1)}, u32[]{:S(2)}, u32[]{:S(2)}) async-start(bf16[512,1,3,256]{3,2,1,0:T(4,128)(2,1)} %bitcast.102), calls=%async_computation.1 | async-start | bytes 2097152 | tf_op jit(solution)/shard_map/all_to_all | solution.py:92
  96.0 100.9 %all-gather.2.cloned.1.call-start = ((), (), s32[]{:S(2)}) async-start(), calls=%async_computation.5 | async-start | bytes 3244032 | tf_op jit(solution)/shard_map/all_gather | solution.py:140
  111.0 0.9 copy-start.4
  112.7 30.3 %copy-start.2 = (f32[64,24,256]{2,1,0:T(8,128)}, f32[64,24,256]{2,1,0:T(8,128)S(1)}, u32[]{:S(2)}) copy-start(f32[64,24,256]{2,1,0:T(8,128)S(1)} %get-tuple-element.100) | copy-start | bytes 4718596
  112.7 0.9 copy-start.10
  112.7 0.9 copy-start.12
  113.6 29.4 %copy-start.11 = (bf16[256,32]{0,1:T(8,128)(2,1)S(1)}, bf16[256,32]{0,1:T(8,128)(2,1)}, u32[]{:S(2)}) copy-start(bf16[256,32]{0,1:T(8,128)(2,1)} %param.26) | copy-start | bytes 49156
  145.3 13.7 %all-to-all-start.4 = ((bf16[8,64,768]{2,1,0:T(8,128)(2,1)}), bf16[8,64,768]{2,1,0:T(8,128)(2,1)S(1)}, u32[]{:S(2)}, u32[]{:S(2)}) async-start(bf16[8,64,768]{2,1,0:T(8,128)(2,1)} %broadcast_in_dim.23), calls=%async_computation.4 | async-start | bytes 1572864 | tf_op jit(solution)/shard_map/all_to_all | solution.py:12
Sparse Core Ops, SparseCore 0:
  143.2 53.7 all-gather.1
where the time goes:
time: 249 us; the launch traced here: 247 us
  waiting for transfers between devices  69 us (28%)
  local copies, waits for them, and re-layouts  60.3 us (24%)
  matrix products  53.5 us (21%)
  blocking collectives  27.5 us (11%)
  between operations  14.3 us (6%)
  starting transfers between devices  13.4 us (5%)
  other arithmetic  9.38 us (4%)
    all_gather x1, waiting for transfers between devices, shards(): lax.all_gather(own_block, 'col', axis=0, tiled=True)  35.4 us
    convert_element_type x1, local copies, waits for them, and re-layouts, shards(): outer_sum = products.reshape(pair_rows, side_width, res_dev, side_width)....  20.1 us
    all_to_all x1, blocking collectives, shards(): lax.all_to_all(left, 'col', split_axis=0, concat_axis=1, tiled=True)  19.5 us
    sub x3, matrix products, column(): weights = jax.nn.softmax(logits, axis=-1).astype(jnp.bfloat16)  15 us
    all_to_all x1, waiting for transfers between devices, shards(): lax.all_to_all(gated_output, 'row', split_axis=0, concat_axis=1, tiled=True)  14 us
    dot_general x1, matrix products, shards(): lax.dot_general(lax.all_gather(own_block, 'col', axis=0, tiled=True), rig...  13.7 us
    dot_general x3, matrix products, column(): jnp.einsum('hst,thd->shd', weights, heads_value, preferred_element_type=j...  12.7 us
    all_to_all x1, waiting for transfers between devices, shards(): lax.all_to_all(normed, 'row', split_axis=1, concat_axis=0, tiled=True)[:, 0]  11.5 us
  transfers between devices with their start and end apart: 4, of which 4 were waited for; matrix products, arithmetic and copies ran while one was open for 3% of the time, Pallas kernels for 0%

commit v1 on v0

--- a/solution.py
+++ b/solution.py
@@ -70,7 +70,10 @@
         ).reshape(sequence_total, hidden)
         return (jax.nn.sigmoid(col_gate) * attended).astype(jnp.bfloat16)
 
-    tokens = lax.all_to_all(normed, "row", split_axis=1, concat_axis=0, tiled=True)[:, 0]
+    tokens = jnp.concatenate(
+        lax.all_to_all(jnp.stack(jnp.split(normed, lax.axis_size("row"), axis=1)), "row", 0, 0),
+        axis=0,
+    )[:, 0]
     residues = tokens.shape[1]
     token_rows = tokens.reshape(-1, channel_width)
     queries = (

time: 249 us -> 261 us (1.048)
  local copies, waits for them, and re-layouts: 60.3 us -> 70.9 us
    reshape x3, local copies, waits for them, and re-layouts: 4.84 us -> 9.9 us  [arrange(): return values.reshape(sequence_total, residues, -1).transpose(1, 0, 2)]
    unnamed x27 -> x34, local copies, waits for them, and re-layouts: 2.5 us -> 7.02 us
where the time goes in v1:
time: 261 us; the launch traced here: 260 us
  local copies, waits for them, and re-layouts  70.9 us (27%)
  waiting for transfers between devices  69.9 us (27%)
  matrix products  54.9 us (21%)
  blocking collectives  27.6 us (11%)
  between operations  14.3 us (5%)
  starting transfers between devices  13.4 us (5%)
  other arithmetic  8.53 us (3%)
    all_gather x1, waiting for transfers between devices, shards(): lax.all_gather(own_block, 'col', axis=0, tiled=True)  36.3 us
    convert_element_type x1, local copies, waits for them, and re-layouts, shards(): outer_sum = products.reshape(pair_rows, side_width, res_dev, side_width)....  20.1 us
    all_to_all x1, blocking collectives, shards(): lax.all_to_all(left, 'col', split_axis=0, concat_axis=1, tiled=True)  19.6 us
    sub x3, matrix products, column(): weights = jax.nn.softmax(logits, axis=-1).astype(jnp.bfloat16)  15.1 us
    dot_general x1, matrix products, shards(): lax.dot_general(lax.all_gather(own_block, 'col', axis=0, tiled=True), rig...  14.5 us
    all_to_all x1, waiting for transfers between devices, shards(): lax.all_to_all(gated_output, 'row', split_axis=0, concat_axis=1, tiled=True)  14 us
    dot_general x3, matrix products, column(): jnp.einsum('hst,thd->shd', weights, heads_value, preferred_element_type=j...  12.7 us
    all_to_all x1, waiting for transfers between devices, shards(): lax.all_to_all(jnp.stack(jnp.split(normed, lax.axis_size('row'), axis=1))...  11.5 us
  transfers between devices with their start and end apart: 4, of which 4 were waited for; matrix products, arithmetic and copies ran while one was open for 3% of the time, Pallas kernels for 0%

profile of v1, /device:TPU:5, one launch (start us, length us, event | category | flops | bytes accessed | tf_op | source)
XLA Modules:
  0.0 259.6 jit_solution(8009710530299399604)
XLA Ops:
  7.2 1.8 reduce_sum.54
  15.7 5.5 %all-to-all-start = ((bf16[8,64,1,3,256]{4,1,3,2,0:T(8,128)(2,1)}), bf16[8,64,1,3,256]{4,1,3,2,0:T(8,128)(2,1)S(1)}, u32[]{:S(2)}, u32[]{:S(2)}) async-start(bf16[8,64,1,3,256]{4,1,3,2,0:T(8,128)(2,1)} %fusion.16), calls=%async_computation | async-start | bytes 1572864 | tf_op jit(solution)/shard_map/all_to_all | solution.py:74
  21.3 11.5 %all-to-all-done = bf16[8,64,1,3,256]{4,1,3,2,0:T(8,128)(2,1)S(1)} async-done(((bf16[8,64,1,3,256]{4,1,3,2,0:T(8,128)(2,1)}), bf16[8,64,1,3,256]{4,1,3,2,0:T(8,128)(2,1)S(1)}, u32[]{:S(2)}, u32[]{:S(2)}) %all-to-all-start) | async-done | bytes 786464 | tf_op jit(solution)/shard_map/all_to_all | solution.py:74
  32.8 1.6 copy.106
  34.4 2.4 reshape_squeeze_reshape.3
  38.1 3.3 %reshape.156 = bf16[512,3,256]{2,1,0:T(4,128)(2,1)} reshape(bf16[1536,256]{1,0:T(8,128)(2,1)} %convolution_convert_fusion.1) | data formatting | bytes 1572864 | tf_op jit(solution)/shard_map/reshape | solution.py:89
  41.4 2.3 copy.108
  45.0 3.3 %reshape.157 = bf16[512,3,256]{2,1,0:T(4,128)(2,1)} reshape(bf16[1536,256]{1,0:T(8,128)(2,1)} %fusion.9) | data formatting | bytes 1572864 | tf_op jit(solution)/shard_map/reshape | solution.py:89
  48.3 2.3 copy.109
  51.8 3.3 %reshape.158 = bf16[512,3,256]{2,1,0:T(4,128)(2,1)} reshape(bf16[1536,256]{1,0:T(8,128)(2,1)} %convolution_convert_fusion) | data formatting | bytes 1572864 | tf_op jit(solution)/shard_map/reshape | solution.py:89
  55.1 2.3 copy.110
  57.5 1.5 convolution_bitcast_fusion
  59.0 40.3 %while.10 = (s32[]{:T(128)}, bf16[3,512,256]{1,2,0:T(8,128)(2,1)}, f32[3,512,256]{2,1,0:T(8,128)}, bf16[3,512,256]{1,2,0:T(8,128)(2,1)}, bf16[3,512,256]{1,2,0:T...) while((s32[]{:T(128)}, bf16[3,512,256]{1,2,0:T(8,128)(2,1)}, ...), condition=%wide.region_5.6_spmd, body=%wide.region_2.5_spmd.sunk | while | flops 279577088 | bytes 23104096 | solution.py:91
  60.0 5.0 %fusion.51 = (f32[8,512]{1,0:T(8,128)S(1)}, f32[8,512,512]{1,2,0:T(8,128)}) fusion(f32[512]{0:T(512)S(1)} %get-tuple-element.174, bf16[512,8,32]{0,2,1:T(8,128)(2,1)S(1)} %bitcast.124, bf16[512,8,32]{0,2,1:T(8,128)(2,1)S(1)} %bitcast.123), kind=kOutput, calls=%fused_computation.62.clone.1 | convolution fusion | flops 140509696 | bytes 8931328 | tf_op jit(solution)/shard_map/while/body/eval_jaxpr/sub | solution.py:67
  66.0 4.2 %fusion.52 = f32[8,32,512]{2,1,0:T(8,128)S(1)} fusion(bf16[512,8,32]{0,2,1:T(8,128)(2,1)S(1)} %bitcast.122, f32[8,512,512]{1,2,0:T(8,128)} %get-tuple-element.150, f32[8,512]{1,0:T(8,128)S(1)} %get-tuple-element.151), kind=kOutput, calls=%fused_computation.6.clone.1 | convolution fusion | flops 138412032 | bytes 9191424 | tf_op jit(solution)/shard_map/while/body/eval_jaxpr/hst,thd->shd/dot_general | solution.py:68
  73.5 5.0 %fusion.51 = (f32[8,512]{1,0:T(8,128)S(1)}, f32[8,512,512]{1,2,0:T(8,128)}) fusion(f32[512]{0:T(512)S(1)} %get-tuple-element.174, bf16[512,8,32]{0,2,1:T(8,128)(2,1)S(1)} %bitcast.124, bf16[512,8,32]{0,2,1:T(8,128)(2,1)S(1)} %bitcast.123), kind=kOutput, calls=%fused_computation.62.clone.1 | convolution fusion | flops 140509696 | bytes 8931328 | tf_op jit(solution)/shard_map/while/body/eval_jaxpr/sub | solution.py:67
  79.5 4.2 %fusion.52 = f32[8,32,512]{2,1,0:T(8,128)S(1)} fusion(bf16[512,8,32]{0,2,1:T(8,128)(2,1)S(1)} %bitcast.122, f32[8,512,512]{1,2,0:T(8,128)} %get-tuple-element.150, f32[8,512]{1,0:T(8,128)S(1)} %get-tuple-element.151), kind=kOutput, calls=%fused_computation.6.clone.1 | convolution fusion | flops 138412032 | bytes 9191424 | tf_op jit(solution)/shard_map/while/body/eval_jaxpr/hst,thd->shd/dot_general | solution.py:68
  86.9 5.0 %fusion.51 = (f32[8,512]{1,0:T(8,128)S(1)}, f32[8,512,512]{1,2,0:T(8,128)}) fusion(f32[512]{0:T(512)S(1)} %get-tuple-element.174, bf16[512,8,32]{0,2,1:T(8,128)(2,1)S(1)} %bitcast.124, bf16[512,8,32]{0,2,1:T(8,128)(2,1)S(1)} %bitcast.123), kind=kOutput, calls=%fused_computation.62.clone.1 | convolution fusion | flops 140509696 | bytes 8931328 | tf_op jit(solution)/shard_map/while/body/eval_jaxpr/sub | solution.py:67
  92.9 4.2 %fusion.52 = f32[8,32,512]{2,1,0:T(8,128)S(1)} fusion(bf16[512,8,32]{0,2,1:T(8,128)(2,1)S(1)} %bitcast.122, f32[8,512,512]{1,2,0:T(8,128)} %get-tuple-element.150, f32[8,512]{1,0:T(8,128)S(1)} %get-tuple-element.151), kind=kOutput, calls=%fused_computation.6.clone.1 | convolution fusion | flops 138412032 | bytes 9191424 | tf_op jit(solution)/shard_map/while/body/eval_jaxpr/hst,thd->shd/dot_general | solution.py:68
  99.3 2.3 copy.111
  101.6 4.3 %all-to-all-start.1 = ((bf16[512,1,3,256]{3,2,1,0:T(4,128)(2,1)}), bf16[512,1,3,256]{3,2,1,0:T(4,128)(2,1)S(1)}, u32[]{:S(2)}, u32[]{:S(2)}) async-start(bf16[512,1,3,256]{3,2,1,0:T(4,128)(2,1)} %bitcast.129), calls=%async_computation.1 | async-start | bytes 2097152 | tf_op jit(solution)/shard_map/all_to_all | solution.py:95
  106.8 14.0 %all-to-all-done.1 = bf16[512,1,3,256]{3,2,1,0:T(4,128)(2,1)S(1)} async-done(((bf16[512,1,3,256]{3,2,1,0:T(4,128)(2,1)}), bf16[512,1,3,256]{3,2,1,0:T(4,128)(2,1)S(1)}, u32[]{:S(2)}, u32[]{:S(2)}) %all-to-all-start.1) | async-done | bytes 786464 | tf_op jit(solution)/shard_map/all_to_all | solution.py:95
  124.7 19.6 %all_to_all.60 = bf16[32,2,768]{2,1,0:T(2,128)(2,1)S(1)} all-to-all(bf16[32,2,768]{2,1,0:T(2,128)(2,1)S(1)} %all_to_all.47), channel_id=1, replica_groups=mesh['row'=8,'col'=32] {'col'}, dimensions={0} | all-to-all | bytes 196608 | tf_op jit(solution)/shard_map/all_to_all | solution.py:140
  144.2 8.1 %all_to_all.61 = bf16[2,8,3072]{2,0,1:T(2,128)(2,1)S(1)} all-to-all(bf16[2,8,3072]{2,0,1:T(2,128)(2,1)S(1)} %bitcast.147), channel_id=1, replica_groups=mesh['row'=8,'col'=32] {'row'}, dimensions={1} | all-to-all | bytes 196608 | tf_op jit(solution)/shard_map/all_to_all | solution.py:141
  155.2 3.5 %all-to-all-start.4 = ((bf16[8,64,768]{2,1,0:T(8,128)(2,1)}), bf16[8,64,768]{2,1,0:T(8,128)(2,1)S(1)}, u32[]{:S(2)}, u32[]{:S(2)}) async-start(bf16[8,64,768]{2,1,0:T(8,128)(2,1)} %broadcast_in_dim.23), calls=%async_computation.4 | async-start | bytes 1572864 | tf_op jit(solution)/shard_map/all_to_all | solution.py:12
  161.0 8.0 %all-to-all-done.4 = bf16[8,64,768]{2,1,0:T(8,128)(2,1)S(1)} async-done(((bf16[8,64,768]{2,1,0:T(8,128)(2,1)}), bf16[8,64,768]{2,1,0:T(8,128)(2,1)S(1)}, u32[]{:S(2)}, u32[]{:S(2)}) %all-to-all-start.4) | async-done | bytes 786464 | tf_op jit(solution)/shard_map/all_to_all | solution.py:12
  170.6 36.3 %all-gather.2.cloned.1.call-done = bf16[512,3072]{1,0:T(8,128)(2,1)} async-done(((bf16[16,3072]{1,0:T(8,128)(2,1)}), bf16[512,3072]{1,0:T(8,128)(2,1)}) %all-gather.2.cloned.1.call-update) | async-done | bytes 3145744 | tf_op jit(solution)/shard_map/all_gather | solution.py:143
  206.9 4.7 %copy.121 = bf16[3072,512]{1,0:T(8,128)(2,1)} copy(bf16[3072,512]{0,1:T(8,128)(2,1)} %bitcast.132) | data formatting | bytes 6291456 | tf_op jit(solution)/shard_map/dot_general | solution.py:142
  211.6 14.5 %convert_bitcast_fusion = bf16[96,24,32,32]{3,2,1,0:T(8,128)(2,1)} fusion(bf16[96,32,512,1]{2,1,3,0:T(8,128)(2,1)} %bitcast.133, bf16[24,32,512,1]{2,1,0,3:T(8,128)(2,1)S(1)} %bitcast.145), kind=kOutput, calls=%fused_computation.15 | convolution fusion | flops 2418278400 | bytes 8650752 | tf_op jit(solution)/shard_map/dot_general | solution.py:142
  226.1 20.1 %copy.127 = bf16[96,24,32,32]{0,3,2,1:T(8,128)(2,1)} copy(bf16[96,24,32,32]{3,2,1,0:T(8,128)(2,1)} %convert_bitcast_fusion) | data formatting | bytes 9437184 | tf_op jit(solution)/shard_map/convert_element_type | solution.py:152
  246.3 4.8 %convolution_divide_fusion = f32[96,24,128]{2,0,1:T(8,128)S(1)} fusion(bf16[96,24,1024]{0,2,1:T(8,128)(2,1)} %bitcast.125, f32[96,24]{0,1:T(8,128)S(1)} %maximum_convert_fusion, bf16[1024,128]{1,0:T(8,128)(2,1)S(1)} %copy-done), kind=kOutput, calls=%fused_computation.27 | convolution fusion | flops 604274688 | bytes 6169600 | tf_op jit(solution)/shard_map/dot_general | solution.py:154
  251.1 1.7 copy.129
  (89 shorter events, 34.3 us)
Async XLA Ops:
  7.2 239.1 %copy-start = (bf16[1024,128]{1,0:T(8,128)(2,1)S(1)}, bf16[1024,128]{1,0:T(8,128)(2,1)}, u32[]{:S(2)}) copy-start(bf16[1024,128]{1,0:T(8,128)(2,1)} %param.27) | copy-start | bytes 786436
  7.2 1.9 copy-start.1
  7.2 2.7 %copy-start.9 = (f32[256]{0:T(256)S(1)}, f32[256]{0:T(256)}, u32[]{:S(2)}) copy-start(f32[256]{0:T(256)} %param.18) | copy-start | bytes 3076
  10.5 10.7 %copy-start.8 = (s32[512]{0:T(512)S(1)}, s32[512]{0:T(512)}, u32[]{:S(2)}) copy-start(s32[512]{0:T(512)} %param.16) | copy-start | bytes 6148
  15.7 17.1 %all-to-all-start = ((bf16[8,64,1,3,256]{4,1,3,2,0:T(8,128)(2,1)}), bf16[8,64,1,3,256]{4,1,3,2,0:T(8,128)(2,1)S(1)}, u32[]{:S(2)}, u32[]{:S(2)}) async-start(bf16[8,64,1,3,256]{4,1,3,2,0:T(8,128)(2,1)} %fusion.16), calls=%async_computation | async-start | bytes 1572864 | tf_op jit(solution)/shard_map/all_to_all | solution.py:74
  21.3 15.6 %copy-start.5 = (bf16[256,256]{1,0:T(8,128)(2,1)S(1)}, bf16[256,256]{1,0:T(8,128)(2,1)}, u32[]{:S(2)}) copy-start(bf16[256,256]{1,0:T(8,128)(2,1)} %param.22) | copy-start | bytes 393220
  38.1 5.6 %copy-start.6 = (bf16[256,256]{1,0:T(8,128)(2,1)S(1)}, bf16[256,256]{1,0:T(8,128)(2,1)}, u32[]{:S(2)}) copy-start(bf16[256,256]{1,0:T(8,128)(2,1)} %param.20) | copy-start | bytes 393220
  45.0 5.6 %copy-start.7 = (bf16[256,256]{1,0:T(8,128)(2,1)S(1)}, bf16[256,256]{1,0:T(8,128)(2,1)}, u32[]{:S(2)}) copy-start(bf16[256,256]{1,0:T(8,128)(2,1)} %param.21) | copy-start | bytes 393220
  55.1 2.4 copy-start.3
  101.6 19.2 %all-to-all-start.1 = ((bf16[512,1,3,256]{3,2,1,0:T(4,128)(2,1)}), bf16[512,1,3,256]{3,2,1,0:T(4,128)(2,1)S(1)}, u32[]{:S(2)}, u32[]{:S(2)}) async-start(bf16[512,1,3,256]{3,2,1,0:T(4,128)(2,1)} %bitcast.129), calls=%async_computation.1 | async-start | bytes 2097152 | tf_op jit(solution)/shard_map/all_to_all | solution.py:95
  105.9 101.0 %all-gather.2.cloned.1.call-start = ((), (), s32[]{:S(2)}) async-start(), calls=%async_computation.5 | async-start | bytes 3244032 | tf_op jit(solution)/shard_map/all_gather | solution.py:143
  120.8 0.9 copy-start.4
  122.6 30.4 %copy-start.2 = (f32[64,24,256]{2,1,0:T(8,128)}, f32[64,24,256]{2,1,0:T(8,128)S(1)}, u32[]{:S(2)}) copy-start(f32[64,24,256]{2,1,0:T(8,128)S(1)} %get-tuple-element.100) | copy-start | bytes 4718596
  122.6 0.9 copy-start.10
  122.6 0.9 copy-start.12
  123.4 29.6 %copy-start.11 = (bf16[256,32]{0,1:T(8,128)(2,1)S(1)}, bf16[256,32]{0,1:T(8,128)(2,1)}, u32[]{:S(2)}) copy-start(bf16[256,32]{0,1:T(8,128)(2,1)} %param.26) | copy-start | bytes 49156
  155.2 13.7 %all-to-all-start.4 = ((bf16[8,64,768]{2,1,0:T(8,128)(2,1)}), bf16[8,64,768]{2,1,0:T(8,128)(2,1)S(1)}, u32[]{:S(2)}, u32[]{:S(2)}) async-start(bf16[8,64,768]{2,1,0:T(8,128)(2,1)} %broadcast_in_dim.23), calls=%async_computation.4 | async-start | bytes 1572864 | tf_op jit(solution)/shard_map/all_to_all | solution.py:12
Sparse Core Ops, SparseCore 0:
  153.1 53.7 all-gather.1
